TPU v7x, 32 devices: a whole 2x2x4 slice. The times are simulated.
32 devices in a mesh: rows: 8 (over z, y), cols: 4 (over x, core).
Axes of the slice: x: 2, y: 2, z: 4, core: 2. Of those that a mesh axis runs over, the one named last changes fastest.
Arguments:
- factor_a: bfloat16 [16384, 48, 48], P('rows'), may hold values from -0.875 to 0.875
- factor_b: bfloat16 [16384, 48, 48], P('rows'), may hold values from -0.046875 to 0.046875
- next_factor: bfloat16 [16384, 48, 48], P(('rows', 'cols')), may hold values from -6 to 6
- sketch_leg: bfloat16 [48, 32], replicated, may hold values from -6 to 6
- sketch_rows: bfloat16 [16384, 32], P('rows', 'cols'), may hold values from -6 to 6
Outputs:
- basis: float32 [32, 16384, 48], P(None, ('rows', 'cols'))
- squeezed: float32 [32, 48], replicated
All inputs are finite; a program needn't handle non-finite values.
Results may differ from a plain program's by a relative error of at most 0.0003.
Values sent between devices are 32-bit elements; how exact they have to be, the bound alone decides.
No kernel may reach another device: no remote copies, remote signals or barrier semaphores. Data moves between devices by JAX's collectives and lax.ppermute only.
A program may use at most 128 MiB of HBM per device.

v0:
```python
import jax
import jax.numpy as jnp
from jax import lax
from jax.sharding import PartitionSpec as P


def per_device(factor_a, factor_b, next_factor, sketch_leg, sketch_rows):
    high = lax.Precision.HIGHEST
    local_rows = factor_a.shape[0]
    width = factor_a.shape[1]
    col_parts = lax.axis_size("cols")
    quarter = local_rows // col_parts
    col_index = lax.axis_index("cols")
    count = local_rows * lax.axis_size("rows") * width
    start = col_index * quarter
    far_part = jnp.einsum("sp,syk->pyk", sketch_rows, factor_b, preferred_element_type=jnp.float32)
    far = lax.psum(far_part, "rows")
    far_all = lax.all_gather(far, "cols", axis=0, tiled=True)
    own_rows = lax.dynamic_slice_in_dim(factor_a, start, quarter, 0)
    near = jnp.einsum("sxk,xp->psk", own_rows, sketch_leg, preferred_element_type=jnp.float32)
    sketch = jnp.einsum("psk,pyk->psy", near, far_all, precision=high)
    columns = sketch.shape[0]
    flat = sketch.reshape(columns, quarter * width)
    own_next = next_factor.reshape(quarter * width, width).astype(jnp.float32)
    gram_part = jnp.dot(flat, flat.T, precision=high)
    root_count = jnp.sqrt(jnp.float32(count))
    gram = lax.psum(gram_part, ("rows", "cols")) / count
    lower = jnp.linalg.cholesky(gram)
    basis = jax.scipy.linalg.solve_triangular(lower, flat, lower=True)
    squeeze_part = jnp.dot(basis, own_next, precision=high)
    squeezed = lax.psum(squeeze_part, ("rows", "cols")) / root_count
    return (basis.reshape(columns, quarter, width), squeezed)


def solution(mesh):
    return jax.shard_map(
        per_device,
        mesh=mesh,
        in_specs=(
            P("rows", None, None),
            P("rows", None, None),
            P(("rows", "cols"), None, None),
            P(),
            P("rows", "cols"),
        ),
        out_specs=(P(None, ("rows", "cols"), None), P()),
        check_vma=False,
    )
```

profile of v0, /device:TPU:0, one launch (start us, length us, event | category | flops | bytes accessed | tf_op | source)
XLA Modules:
  0.0 238.8 jit_solution(5856863479625042245)
XLA Ops:
  7.2 0.7 copy-done
  7.9 8.9 %fusion.12 = f32[8,48,48]{2,0,1:T(8,128)} fusion(bf16[2048,48,48]{0,2,1:T(8,128)(2,1)} %param.6, bf16[2048,8]{0,1:T(8,128)(2,1)S(1)} %copy-done), kind=kOutput, calls=%fused_computation.8 | convolution fusion | flops 75497472 | bytes 9543680 | tf_op jit(solution)/shard_map/sp,syk->pyk/dot_general | solution.py:16
  16.9 1.8 constant_dynamic-slice_fusion
  18.7 3.4 %fusion.6 = f32[32,512,48]{1,0,2:T(8,128)} fusion(bf16[512,48,48]{0,2,1:T(8,128)(2,1)S(1)} %constant_dynamic-slice_fusion, bf16[48,32]{0,1:T(8,128)(2,1)S(1)} %copy-done.2), kind=kOutput, calls=%fused_computation.6 | convolution fusion | flops 75497472 | bytes 5508096 | tf_op jit(solution)/shard_map/sxk,xp->psk/dot_general | solution.py:20
  22.1 5.0 %copy.27 = bf16[512,48,48]{1,0,2:T(8,128)(2,1)} copy(bf16[512,48,48]{0,2,1:T(8,128)(2,1)S(1)} %copy-done.1) | data formatting | bytes 4718592 | tf_op args[2]
  27.2 14.0 %reshape.25 = bf16[24576,48]{0,1:T(8,128)(2,1)} reshape(bf16[512,48,48]{1,0,2:T(8,128)(2,1)} %copy.27) | data formatting | bytes 4718592 | tf_op jit(solution)/shard_map/reshape | solution.py:24
  41.1 49.3 %all-reduce.2.cloned.1.call-done = f32[8,48,48]{2,0,1:T(8,128)} async-done(((f32[8,48,48]{2,0,1:T(8,128)}), f32[8,48,48]{2,0,1:T(8,128)}) %all-reduce.2.cloned.1.call-update) | async-done | bytes 73744 | tf_op jit(solution)/shard_map/psum | solution.py:17
  90.4 1.0 copy.20
  91.4 8.8 %all_gather.3 = f32[32,48,48]{2,1,0:T(8,128)S(1)} all-gather(f32[8,48,48]{2,1,0:T(8,128)S(1)} %copy.20), channel_id=1, replica_groups=mesh['rows'=8,'cols'=4] {'cols'}, dimensions={0}, use_global_device_ids=true | all-gather | bytes 368640 | tf_op jit(solution)/shard_map/all_gather | solution.py:18
  100.1 6.7 %fusion.2 = f32[32,512,48]{1,2,0:T(8,128)S(1)} fusion(f32[32,48,48]{2,1,0:T(8,128)S(1)} %all_gather.3, f32[32,512,48]{1,0,2:T(8,128)} %fusion.6), kind=kOutput, calls=%fused_computation.2 | convolution fusion | flops 452984832 | bytes 6586368 | tf_op jit(solution)/shard_map/psk,pyk->psy/dot_general | solution.py:21
  106.9 4.2 %fusion.9 = f32[32,32]{0,1:T(8,128)S(1)} fusion(f32[32,512,48]{1,2,0:T(8,128)S(1)} %fusion.2), kind=kOutput, calls=%fused_computation.7 | convolution fusion | flops 301989888 | bytes 3149824 | tf_op jit(solution)/shard_map/dot_general | solution.py:25
  111.1 4.7 %copy.26 = f32[32,512,48]{2,1,0:T(8,128)} copy(f32[32,512,48]{1,2,0:T(8,128)S(1)} %fusion.2) | data formatting | bytes 6291456 | tf_op jit(solution)/shard_map/psk,pyk->psy/dot_general | solution.py:21
  115.8 38.7 %psum.22 = f32[32,32]{0,1:T(8,128)S(1)} all-reduce(f32[32,32]{0,1:T(8,128)S(1)} %fusion.9), channel_id=1, replica_groups=mesh['rows'=8,'cols'=4] {'rows','cols'}, use_global_device_ids=true, to_apply=%region_1.0 | all-reduce | flops 1024 | bytes 8192 | tf_op jit(solution)/shard_map/psum | solution.py:27
  154.5 2.9 %cholesky.16 = f32[32,32]{1,0:T(8,128)S(1)} custom-call(f32[32,32]{1,0:T(8,128)S(1)} %fusion.17), custom_call_target="Cholesky" | custom-call | tf_op jit(solution)/shard_map/jit(cholesky)/cholesky | solution.py:28
  157.5 0.6 compare_reduce_fusion
  158.1 0.7 fusion.14
  158.8 2.4 %custom-call.7 = f32[1,32,32]{1,2,0:T(8,128)S(1)} custom-call(f32[1,32,32]{2,1,0:T(8,128)S(1)} %fusion.14), custom_call_target="InvertDiagBlocksLowerTriangular" | custom-call | tf_op jit(solution)/shard_map/jit(_solve_triangular)/triangular_solve | solution.py:29
  161.2 9.8 %reshape.23 = f32[32,24576]{1,0:T(8,128)} reshape(f32[32,512,48]{2,1,0:T(8,128)} %copy.26) | data formatting | bytes 6291456 | tf_op jit(solution)/shard_map/reshape | solution.py:23
  171.0 4.6 %fusion.15 = f32[32,24576]{1,0:T(8,128)S(1)} fusion(f32[32,24576]{1,0:T(8,128)} %reshape.23, f32[1,32,32]{1,2,0:T(8,128)S(1)} %custom-call.7), kind=kOutput, calls=%fused_computation.12 | convolution fusion | flops 301989888 | bytes 6295552 | tf_op jit(solution)/shard_map/jit(_solve_triangular)/triangular_solve | solution.py:29
  175.6 5.4 %reshape.24 = f32[32,512,48]{2,1,0:T(8,128)} reshape(f32[32,24576]{1,0:T(8,128)S(1)} %fusion.15) | data formatting | bytes 6291456 | tf_op jit(solution)/shard_map/reshape | solution.py:32
  181.0 3.7 %fusion.19 = f32[32,48]{1,0:T(8,128)S(1)} fusion(f32[32,24576]{1,0:T(8,128)S(1)} %fusion.15, bf16[24576,48]{0,1:T(8,128)(2,1)} %reshape.25), kind=kOutput, calls=%fused_computation.24 | convolution fusion | flops 452984832 | bytes 5511168 | tf_op jit(solution)/shard_map/dot_general | solution.py:30
  184.7 40.1 %psum.23 = f32[32,48]{1,0:T(8,128)S(1)} all-reduce(f32[32,48]{1,0:T(8,128)S(1)} %fusion.19), channel_id=1, replica_groups=mesh['rows'=8,'cols'=4] {'rows','cols'}, use_global_device_ids=true, to_apply=%region_4.5 | all-reduce | flops 1536 | bytes 12288 | tf_op jit(solution)/shard_map/psum | solution.py:31
  224.8 0.6 broadcast_multiply_fusion
  225.5 6.5 %copy.28 = f32[32,512,48]{1,2,0:T(8,128)} copy(f32[32,512,48]{2,1,0:T(8,128)} %reshape.24) | data formatting | bytes 6291456
  (11 shorter events, 0.2 us)
Async XLA Ops:
  7.2 0.8 copy-start
  7.2 83.2 %all-reduce.2.cloned.1.call-start = ((), (), s32[]{:S(2)}) async-start(), calls=%async_computation | async-start | bytes 393216 | tf_op jit(solution)/shard_map/psum | solution.py:17
  16.8 1.9 copy-start.2
  18.7 3.4 %copy-start.1 = (bf16[512,48,48]{0,2,1:T(8,128)(2,1)S(1)}, bf16[512,48,48]{0,2,1:T(8,128)(2,1)}, u32[]{:S(2)}) copy-start(bf16[512,48,48]{0,2,1:T(8,128)(2,1)} %param.7) | copy-start | bytes 7077892
Sparse Core Ops, SparseCore 0:
  17.0 73.3 all-reduce.1
where the time goes:
time: 239 us
  blocking collectives  87.6 us (37%)
  waiting for transfers between devices  49.3 us (21%)
  local copies, waits for them, and re-layouts  48.9 us (20%)
  matrix products  31.5 us (13%)
  between operations  14.1 us (6%)
  other arithmetic  7.3 us (3%)
    psum x1, waiting for transfers between devices, per_device(): far = lax.psum(far_part, 'rows')  49.3 us
    psum x1, blocking collectives, per_device(): squeezed = lax.psum(squeeze_part, ('rows', 'cols')) / root_count  40.1 us
    psum x1, blocking collectives, per_device(): gram = lax.psum(gram_part, ('rows', 'cols')) / count  38.7 us
    reshape x1, local copies, waits for them, and re-layouts, per_device(): own_next = next_factor.reshape(quarter * width, width).astype(jnp.float32)  14 us
    unnamed x8, local copies, waits for them, and re-layouts  12.3 us
    reshape x1, local copies, waits for them, and re-layouts, per_device(): flat = sketch.reshape(columns, quarter * width)  9.77 us
    dot_general x1, matrix products, per_device(): jnp.einsum('sp,syk->pyk', sketch_rows, factor_b, preferred_element_type=j...  8.91 us
    all_gather x1, blocking collectives, per_device(): far_all = lax.all_gather(far, 'cols', axis=0, tiled=True)  8.76 us
  transfers between devices with their start and end apart: 1, of which 1 were waited for; matrix products, arithmetic and copies ran while one was open for 10% of the time, Pallas kernels for 0%

commit v1 on v0

--- a/solution.py
+++ b/solution.py
@@ -14,7 +14,7 @@
     count = local_rows * lax.axis_size("rows") * width
     start = col_index * quarter
     far_part = jnp.einsum("sp,syk->pyk", sketch_rows, factor_b, preferred_element_type=jnp.float32)
-    far = lax.psum(far_part, "rows")
+    far = jnp.sum(lax.all_gather(far_part, "rows"), axis=0)
     far_all = lax.all_gather(far, "cols", axis=0, tiled=True)
     own_rows = lax.dynamic_slice_in_dim(factor_a, start, quarter, 0)
     near = jnp.einsum("sxk,xp->psk", own_rows, sketch_leg, preferred_element_type=jnp.float32)

time: 239 us -> 211 us (0.88)
  waiting for transfers between devices: 49.3 us -> 0 us
  blocking collectives: 87.6 us -> 126 us
  between operations: 14.1 us -> 0.73 us
  matrix products: 31.5 us -> 26.1 us
    psum x1 -> x0, waiting for transfers between devices: 49.3 us -> none  [per_device(): far = lax.psum(far_part, 'rows')]
    all_gather x0 -> x1, blocking collectives: none -> 38.7 us  [per_device(): far = jnp.sum(lax.all_gather(far_part, 'rows'), axis=0)]
  transfers between devices with their start and end apart: 1 -> 0, of which waited for: 1 -> 0; matrix products, arithmetic and copies ran while one was open for 10% -> 0% of each run, Pallas kernels for 0% -> 0%
where the time goes in v1:
time: 211 us; the launch traced here: 210 us
  blocking collectives  126 us (60%)
  local copies, waits for them, and re-layouts  49.8 us (24%)
  matrix products  26.1 us (12%)
  other arithmetic  7.47 us (4%)
    psum x1, blocking collectives, per_device(): squeezed = lax.psum(squeeze_part, ('rows', 'cols')) / root_count  41 us
    all_gather x1, blocking collectives, per_device(): far = jnp.sum(lax.all_gather(far_part, 'rows'), axis=0)  38.7 us
    psum x1, blocking collectives, per_device(): gram = lax.psum(gram_part, ('rows', 'cols')) / count  37.8 us
    unnamed x8, local copies, waits for them, and re-layouts  14.1 us
    reshape x1, local copies, waits for them, and re-layouts, per_device(): own_next = next_factor.reshape(quarter * width, width).astype(jnp.float32)  13.9 us
    reshape x1, local copies, waits for them, and re-layouts, per_device(): flat = sketch.reshape(columns, quarter * width)  9.74 us
    all_gather x1, blocking collectives, per_device(): far_all = lax.all_gather(far, 'cols', axis=0, tiled=True)  8.6 us
    dot_general x1, matrix products, per_device(): jnp.einsum('sp,syk->pyk', sketch_rows, factor_b, preferred_element_type=j...  7 us

profile of v1, /device:TPU:0, one launch (start us, length us, event | category | flops | bytes accessed | tf_op | source)
XLA Modules:
  0.0 210.2 jit_solution(11933045794093815620)
XLA Ops:
  0.7 0.7 copy-done
  1.4 7.0 %fusion.12 = f32[8,48,48]{2,0,1:T(8,128)S(1)} fusion(bf16[2048,48,48]{0,2,1:T(8,128)(2,1)} %param.6, bf16[2048,8]{0,1:T(8,128)(2,1)S(1)} %copy-done), kind=kOutput, calls=%fused_computation.9 | convolution fusion | flops 75497472 | bytes 9543680 | tf_op jit(solution)/shard_map/sp,syk->pyk/dot_general | solution.py:16
  8.4 38.7 %all-gather = f32[64,48,48]{2,0,1:T(8,128)S(1)} all-gather(f32[8,48,48]{2,0,1:T(8,128)S(1)} %fusion.12), channel_id=2, replica_groups=mesh['rows'=8,'cols'=4] {'rows'}, dimensions={0}, use_global_device_ids=true | all-gather | bytes 663552 | tf_op jit(solution)/shard_map/all_gather | solution.py:17
  47.1 0.2 bitcast_reduce_fusion
  47.4 8.6 %all_gather.11 = f32[32,48,48]{2,1,0:T(8,128)S(1)} all-gather(f32[8,48,48]{2,1,0:T(8,128)S(1)} %copy.20), channel_id=1, replica_groups=mesh['rows'=8,'cols'=4] {'cols'}, dimensions={0}, use_global_device_ids=true | all-gather | bytes 368640 | tf_op jit(solution)/shard_map/all_gather | solution.py:18
  56.0 1.8 constant_dynamic-slice_fusion
  57.8 1.7 fusion.6
  59.5 4.9 %fusion.2 = f32[32,512,48]{1,2,0:T(8,128)S(1)} fusion(f32[32,48,48]{2,1,0:T(8,128)S(1)} %all_gather.11, f32[32,512,48]{1,0,2:T(8,128)S(1)} %fusion.6), kind=kOutput, calls=%fused_computation.2 | convolution fusion | flops 452984832 | bytes 6586368 | tf_op jit(solution)/shard_map/psk,pyk->psy/dot_general | solution.py:21
  64.4 4.2 %fusion.9 = f32[32,32]{0,1:T(8,128)S(1)} fusion(f32[32,512,48]{1,2,0:T(8,128)S(1)} %fusion.2), kind=kOutput, calls=%fused_computation.8 | convolution fusion | flops 301989888 | bytes 3149824 | tf_op jit(solution)/shard_map/dot_general | solution.py:25
  68.6 37.8 %psum.14 = f32[32,32]{0,1:T(8,128)S(1)} all-reduce(f32[32,32]{0,1:T(8,128)S(1)} %fusion.9), channel_id=1, replica_groups=mesh['rows'=8,'cols'=4] {'rows','cols'}, use_global_device_ids=true, to_apply=%region_1.0 | all-reduce | flops 1024 | bytes 8192 | tf_op jit(solution)/shard_map/psum | solution.py:27
  106.5 2.9 %cholesky.16 = f32[32,32]{1,0:T(8,128)S(1)} custom-call(f32[32,32]{1,0:T(8,128)S(1)} %fusion.17), custom_call_target="Cholesky" | custom-call | tf_op jit(solution)/shard_map/jit(cholesky)/cholesky | solution.py:28
  109.4 0.6 compare_reduce_fusion
  110.1 0.7 fusion.14
  110.7 2.4 %custom-call.7 = f32[1,32,32]{1,2,0:T(8,128)S(1)} custom-call(f32[1,32,32]{2,1,0:T(8,128)S(1)} %fusion.14), custom_call_target="InvertDiagBlocksLowerTriangular" | custom-call | tf_op jit(solution)/shard_map/jit(_solve_triangular)/triangular_solve | solution.py:29
  113.2 4.7 %copy.26 = f32[32,512,48]{2,1,0:T(8,128)} copy(f32[32,512,48]{1,2,0:T(8,128)S(1)} %fusion.2) | data formatting | bytes 6291456 | tf_op jit(solution)/shard_map/psk,pyk->psy/dot_general | solution.py:21
  117.9 9.7 %reshape.23 = f32[32,24576]{1,0:T(8,128)} reshape(f32[32,512,48]{2,1,0:T(8,128)} %copy.26) | data formatting | bytes 6291456 | tf_op jit(solution)/shard_map/reshape | solution.py:23
  127.7 4.6 %fusion.15 = f32[32,24576]{1,0:T(8,128)S(1)} fusion(f32[32,24576]{1,0:T(8,128)} %reshape.23, f32[1,32,32]{1,2,0:T(8,128)S(1)} %custom-call.7), kind=kOutput, calls=%fused_computation.13 | convolution fusion | flops 301989888 | bytes 6295552 | tf_op jit(solution)/shard_map/jit(_solve_triangular)/triangular_solve | solution.py:29
  132.3 6.8 %copy.27 = bf16[512,48,48]{1,0,2:T(8,128)(2,1)} copy(bf16[512,48,48]{0,2,1:T(8,128)(2,1)} %param.7) | data formatting | bytes 4718592 | tf_op args[2]
  139.1 13.9 %reshape.25 = bf16[24576,48]{0,1:T(8,128)(2,1)} reshape(bf16[512,48,48]{1,0,2:T(8,128)(2,1)} %copy.27) | data formatting | bytes 4718592 | tf_op jit(solution)/shard_map/reshape | solution.py:24
  153.1 3.7 %fusion.19 = f32[32,48]{1,0:T(8,128)S(1)} fusion(f32[32,24576]{1,0:T(8,128)S(1)} %fusion.15, bf16[24576,48]{0,1:T(8,128)(2,1)} %reshape.25), kind=kOutput, calls=%fused_computation.25 | convolution fusion | flops 452984832 | bytes 5511168 | tf_op jit(solution)/shard_map/dot_general | solution.py:30
  156.7 41.0 %psum.15 = f32[32,48]{1,0:T(8,128)S(1)} all-reduce(f32[32,48]{1,0:T(8,128)S(1)} %fusion.19), channel_id=1, replica_groups=mesh['rows'=8,'cols'=4] {'rows','cols'}, use_global_device_ids=true, to_apply=%region_4.5 | all-reduce | flops 1536 | bytes 12288 | tf_op jit(solution)/shard_map/psum | solution.py:31
  197.7 0.6 broadcast_multiply_fusion
  198.3 5.4 %reshape.24 = f32[32,512,48]{2,1,0:T(8,128)} reshape(f32[32,24576]{1,0:T(8,128)S(1)} %fusion.15) | data formatting | bytes 6291456 | tf_op jit(solution)/shard_map/reshape | solution.py:32
  203.7 6.5 %copy.28 = f32[32,512,48]{1,2,0:T(8,128)} copy(f32[32,512,48]{2,1,0:T(8,128)} %reshape.24) | data formatting | bytes 6291456
  (10 shorter events, 0.2 us)
Async XLA Ops:
  0.6 0.8 copy-start
  47.3 10.5 %copy-start.2 = (bf16[48,32]{0,1:T(8,128)(2,1)S(1)}, bf16[48,32]{0,1:T(8,128)(2,1)}, u32[]{:S(2)}) copy-start(bf16[48,32]{0,1:T(8,128)(2,1)} %param.8) | copy-start | bytes 9220
  198.3 11.9 %copy-start.1 = (bf16[2048,8]{0,1:T(8,128)(2,1)S(1)}, bf16[2048,8]{0,1:T(8,128)(2,1)}, u32[]{:S(2)}) copy-start(bf16[2048,8]{0,1:T(8,128)(2,1)} %param.9) | copy-start | bytes 98308
